TPU v7x, 32 devices: a whole 2x2x4 slice. The times are simulated.
32 devices in a mesh: row: 8 (over y, x, core), col: 4 (over z).
Axes of the slice: x: 2, y: 2, z: 4, core: 2. Of those that a mesh axis runs over, the one named last changes fastest.
Arguments:
- integrals: bfloat16 [320, 32, 4096], P('row', None, 'col'), may hold values from -6 to 6
- coeffs: bfloat16 [10240, 4096], P('row', 'col'), may hold values from -0.078125 to 0.078125
- mask: int32 [320, 4], replicated, may hold values from 0 to 1, as said below
- offsets: int32 [321], replicated, may hold values from 0 to 7680, as said below
- atom_of_slot: int32 [320], replicated, may hold values from 0 to 319, as said below
Outputs:
- half_transformed: bfloat16 [4096, 4096], P('row', 'col')
Inputs may be any that keep to these rules, and one draw needn't show every extreme that they name: `mask`: 1 marks a significant pair of an atom and a block of 64 window functions. offsets[0] = 0 and offsets[a + 1] - offsets[a] is atom a's number of basis functions, 16 to 32; atoms 2k and 2k + 1 together have 3 * 16; rows of an atom's padded block past its number are padding. `atom_of_slot`: a permutation of the atoms; slot k is held by atom owner k // 40 along row, and atom a's AO-row owner is a // 40; one atom owner holds at least one and at most 5 atoms of any one AO-row owner, and exactly 5 for some pairs.
All inputs are finite; a program needn't handle non-finite values.
Results may differ from a plain program's by a relative error of at most 0.015.
Values may be sent and summed in bfloat16 or wider, within the bound.
A program may use at most 256 MiB of HBM per device.

v0:
```python
import functools

import jax
import jax.numpy as jnp
from jax import lax
from jax.experimental import pallas as pl
from jax.experimental.pallas import tpu as pltpu
from jax.sharding import PartitionSpec as P

MESH = pl.DeviceIdType.MESH
F32 = jnp.float32
BF16 = jnp.bfloat16


def remote(src, dst, send, recv, device):
    return pltpu.make_async_remote_copy(
        src_ref=src, dst_ref=dst, send_sem=send, recv_sem=recv, device_id=device, device_id_type=MESH
    )


def nearest(me, n, s):
    m = jnp.minimum(me, n - 1 - me)
    step = (s + 1) // 2
    near = jnp.where(s % 2 == 1, me - step, me + step)
    far = jnp.where(me <= n - 1 - me, s, n - 1 - s)
    return jnp.where(s <= 2 * m, near, far)


def kernel(
    n_row, n_col, cap, chunks, width,
    meta, integrals, coeffs, out,
    asend, arecv, kept, gathered, mine1, send1, recv1, sums, kept_end, mine4, send4, recv4, relay, pair,
    a_ss, a_rs, r_ss, l_ss, g_rs, s1_ss, s1_rs, s2_ss, s2_rs, k_ss, k_rs, s4_ss, s4_rs, s3_ss, s3_rs, s5_ss, s5_rs, s6_rs,
):
    me = lax.axis_index("row")
    plane = lax.axis_index("col")
    core = me % 2
    chip = me // 2
    n_chip = n_row // 2
    partner = me + 1 - 2 * core
    per_dev, atom_w, row_width = integrals.shape
    half = atom_w // 2
    pairs = per_dev // 2
    packed = 3 * half
    slots = n_row * cap
    per_plane = n_row // n_col
    chips_plane = per_plane // 2
    block = width * chunks
    pick0, len0, sig0 = slots, slots + per_dev, slots + 2 * per_dev
    has_left = plane > 0
    has_right = plane < n_col - 1

    share = n_col >= 4
    pieces = chunks
    piece = row_width // pieces
    is_end = ((plane == 0) | (plane == n_col - 1)) & share
    is_helper = ((plane == 1) | (plane == n_col - 2)) & share
    low_half = plane <= n_col - 1 - plane
    end_plane = jnp.where(low_half, 0, n_col - 1)
    helper_plane = jnp.where(low_half, 1, n_col - 2)

    barrier = pltpu.get_barrier_semaphore()
    for other in range(1, n_row):
        pl.semaphore_signal(barrier, inc=1, device_id=((me + other) % n_row, plane), device_id_type=MESH)

    @pl.when(has_left)
    def _():
        pl.semaphore_signal(barrier, inc=1, device_id=(me, plane - 1), device_id_type=MESH)

    @pl.when(has_right)
    def _():
        pl.semaphore_signal(barrier, inc=1, device_id=(me, plane + 1), device_id_type=MESH)

    def selection(p, weighted):
        s = lax.broadcasted_iota(jnp.int32, (packed, 2 * atom_w), 0)
        t = lax.broadcasted_iota(jnp.int32, (packed, 2 * atom_w), 1)
        extra = meta[len0 + 2 * p] - half
        source = jnp.where(
            s < half, s, jnp.where(s < 2 * half, s + half, jnp.where(s - 2 * half < extra, s - half, s + half - extra))
        )
        hit = source == t
        if weighted:
            sig = jnp.where(t < atom_w, meta[sig0 + 2 * p], meta[sig0 + 2 * p + 1])
            hit = hit & (sig > 0)
        return jnp.where(hit, 1.0, 0.0).astype(BF16)

    def pack_coeffs(p, carry):
        rows = coeffs[pl.ds(pl.multiple_of(p * 2 * atom_w, 2 * atom_w), 2 * atom_w), :]
        live = jnp.dot(selection(p, False), rows, preferred_element_type=F32).astype(BF16)
        at = pl.ds(pl.multiple_of(p * packed, 16), packed)
        for k in range(chunks):
            for b in range(per_plane):
                lo = b * block + k * width
                gathered[plane, k, at, b * width : (b + 1) * width] = live[:, lo : lo + width]
        return carry

    lax.fori_loop(0, pairs, pack_coeffs, 0)
    pl.semaphore_wait(barrier, n_row - 1 + has_left.astype(jnp.int32) + has_right.astype(jnp.int32))

    def to_right(z, k):
        return remote(gathered.at[z, k], gathered.at[z, k], r_ss.at[z, k], g_rs.at[z, k], (me, plane + 1))

    def to_left(z, k):
        return remote(gathered.at[z, k], gathered.at[z, k], l_ss.at[z, k], g_rs.at[z, k], (me, plane - 1))

    def goes_right(z):
        ok = (z <= plane) & has_right
        return ok & ((plane != n_col - 2) | (z == plane)) if share else ok

    def goes_left(z):
        ok = (z >= plane) & has_left
        return ok & ((plane != 1) | (z == plane)) if share else ok

    def forward(z, k):
        @pl.when(goes_right(z))
        def _():
            to_right(z, k).start()

        @pl.when(goes_left(z))
        def _():
            to_left(z, k).start()

    for k in range(chunks):
        forward(plane, k)

    def a_copy(owner):
        return remote(asend.at[owner], arecv.at[me], a_ss.at[owner], a_rs.at[me], (owner, plane))

    def place(step, carry):
        owner = (me + step) % n_row

        @pl.when(step > 0)
        def _():
            for c in range(cap):
                asend[owner, c] = integrals[meta[owner * cap + c]]
            a_copy(owner).start()

        @pl.when(step == 0)
        def _():
            for c in range(cap):
                arecv[me, c] = integrals[meta[me * cap + c]]

        return carry

    lax.fori_loop(0, n_row, place, 0)

    def wait_blocks(step, carry):
        source = (me + step) % n_row
        remote(asend.at[source], arecv.at[source], a_ss.at[source], a_rs.at[source], (source, plane)).wait_recv()
        return carry

    lax.fori_loop(1, n_row, wait_blocks, 0)

    def pack_kept(p, carry):
        first, second = meta[pick0 + 2 * p], meta[pick0 + 2 * p + 1]
        rows = jnp.concatenate([arecv[first // cap, first % cap], arecv[second // cap, second % cap]], axis=0)
        live = jnp.dot(selection(p, True), rows, preferred_element_type=F32).astype(BF16)
        kept[pl.ds(pl.multiple_of(p * packed, 16), packed), :] = live
        return carry

    lax.fori_loop(0, pairs, pack_kept, 0)

    def piece_at(q):
        return pl.ds(pl.multiple_of(q * piece, 128), piece)

    def kept_copy(q):
        return remote(
            kept.at[:, piece_at(q)], kept_end.at[:, piece_at(q)], k_ss.at[q], k_rs.at[q], (me, helper_plane)
        )

    if share:

        @pl.when(is_end)
        def _():
            for q in range(pieces):
                kept_copy(q).start()

    def core_copy(z, k):
        return remote(send1.at[z, k], recv1.at[z, k], s1_ss.at[z, k], s1_rs.at[z, k], (partner, plane))

    def chip_copy(target, k):
        return remote(
            mine1.at[target, k], sums.at[chip, k], s2_ss.at[target, k], s2_rs.at[chip, k], (2 * target + core, plane)
        )

    steps = jnp.where(is_end, 2 * chunks, n_col * chunks)

    def finish(n):
        z = nearest(plane, n_col, n // chunks)
        k = n % chunks
        core_copy(z, k).wait_recv()
        for j in range(chips_plane):
            target = z * chips_plane + j
            both = mine1[target, k].astype(F32) + recv1[z, k, j].astype(F32)

            @pl.when(target == chip)
            def _():
                sums[target, k] = both.astype(BF16)

            @pl.when(target != chip)
            def _():
                mine1[target, k] = both.astype(BF16)
                chip_copy(target, k).start()

    near = (n_col - 3) * chunks

    def begin(t):
        return near * t + t * t

    def decode(e):
        e = jnp.asarray(e, jnp.int32)
        t = jnp.int32(0)
        for w in range(1, chunks):
            t += (e >= begin(w)).astype(jnp.int32)
        u = e - begin(t)
        last = u >= near
        v = u - near
        early = v <= t
        far = jnp.where(last, n_col - 3, u // chunks)
        k = jnp.where(last, jnp.where(early, v, t), u % chunks)
        q = jnp.where(last & (v > t), v - 1 - t, t)
        z = jnp.where(low_half, far + 2, n_col - 3 - far)
        return far, z, k, q

    def far_core_copy(far, k, q):
        return remote(
            send4.at[far, k, q], recv4.at[far, k, q], s4_ss.at[far, k, q], s4_rs.at[far, k, q], (partner, plane)
        )

    def far_copy(far, k, q):
        return remote(
            mine4.at[far, k, q], relay.at[far, k, q], s3_ss.at[far, k, q], s3_rs.at[far, k, q], (me, end_plane)
        )

    def relay_copy(far, j, k, q, target):
        return remote(
            relay.at[far, k, q, j], sums.at[chip, k, :, piece_at(q)], s5_ss.at[far, k, q, j], s5_rs.at[chip, k, q],
            (2 * target + core, plane),
        )

    buddy = chip + 1 - 2 * (chip % 2)

    def pair_copy(far, j, k, q):
        return remote(
            relay.at[far, k, q, j], pair.at[far, k, q, j], s5_ss.at[far, k, q, j], s6_rs.at[far, k, q, j],
            (2 * buddy + core, plane),
        )

    def far_start(e):
        far, z, k, q = decode(e)

        part = lax.dot_general(
            gathered[z, k], kept_end[:, piece_at(q)], (((0,), (0,)), ((), ())), preferred_element_type=F32
        ).astype(BF16)
        for j in range(chips_plane):
            lower = part[2 * j * width : (2 * j + 1) * width]
            upper = part[(2 * j + 1) * width : (2 * j + 2) * width]
            is_lower = core == 0
            mine4[far, k, q, j] = jnp.where(is_lower, lower, upper)
            send4[far, k, q, j] = jnp.where(is_lower, upper, lower)
        far_core_copy(far, k, q).start()

    def far_finish(e):
        far, z, k, q = decode(e)
        far_core_copy(far, k, q).wait_recv()
        for j in range(chips_plane):
            both = mine4[far, k, q, j].astype(F32) + recv4[far, k, q, j].astype(F32)
            mine4[far, k, q, j] = both.astype(BF16)
        far_copy(far, k, q).start()

    def step_body(n, carry):
        @pl.when(n < steps)
        def _():
            z = nearest(plane, n_col, n // chunks)
            k = n % chunks

            @pl.when(z != plane)
            def _():
                to_right(z, k).wait_recv()
                forward(z, k)

            part = lax.dot_general(
                gathered[z, k], kept[...], (((0,), (0,)), ((), ())), preferred_element_type=F32
            ).astype(BF16)
            for j in range(chips_plane):
                lower = part[2 * j * width : (2 * j + 1) * width]
                upper = part[(2 * j + 1) * width : (2 * j + 2) * width]
                is_lower = core == 0
                mine1[z * chips_plane + j, k] = jnp.where(is_lower, lower, upper)
                send1[z, k, j] = jnp.where(is_lower, upper, lower)
            core_copy(z, k).start()

        @pl.when(n > 0)
        def _():
            finish(n - 1)

        if share:
            t = n - (n_col - 1) * chunks

            @pl.when(is_helper & (t >= 0) & (t < chunks))
            def _():
                kept_copy(t).wait_recv()

                def far_body(e, carry):
                    far_start(e)

                    @pl.when(e > 0)
                    def _():
                        far_finish(e - 1)

                    return carry

                lax.fori_loop(begin(t), begin(t + 1), far_body, 0)

        return carry

    lax.fori_loop(0, steps + 1, step_body, 0)
    if share:

        @pl.when(is_helper)
        def _():
            far_finish(begin(chunks) - 1)

        @pl.when(is_end)
        def _():
            def pass_on(e, carry):
                far, z, k, q = decode(e)
                far_copy(far, k, q).wait_recv()
                for j in range(chips_plane):
                    target = z * chips_plane + j

                    @pl.when(target % 2 != chip % 2)
                    def _():
                        pair_copy(far, j, k, q).start()

                    @pl.when(target % 2 == chip % 2)
                    def _():
                        pair_copy(far, j, k, q).wait_recv()
                        both = (relay[far, k, q, j].astype(F32) + pair[far, k, q, j].astype(F32)).astype(BF16)

                        @pl.when(target == chip)
                        def _():
                            sums[target, k, :, piece_at(q)] = both

                        @pl.when(target != chip)
                        def _():
                            relay[far, k, q, j] = both
                            relay_copy(far, j, k, q, target).start()

                return carry

            lax.fori_loop(0, begin(chunks), pass_on, 0)

    my_plane = chip // chips_plane
    distance = jnp.where(low_half, my_plane, n_col - 1 - my_plane)
    from_helper = is_end & (distance >= 2)

    @pl.when(jnp.logical_not(from_helper))
    def _():
        def wait_sums(step, carry):
            source = (chip + step) % n_chip
            for k in range(chunks):
                remote(
                    mine1.at[source, k], sums.at[source, k], s2_ss.at[source, k], s2_rs.at[source, k],
                    (2 * source + core, plane),
                ).wait_recv()
            return carry

        lax.fori_loop(1, n_chip, wait_sums, 0)

    if share:

        @pl.when(from_helper)
        def _():
            def wait_far(step, carry):
                source = (chip + 2 * step) % n_chip
                for k in range(chunks):
                    for q in range(pieces):
                        remote(
                            relay.at[0, k, q, 0], sums.at[source, k, :, piece_at(q)], s5_ss.at[0, k, q, 0],
                            s5_rs.at[source, k, q], (2 * source + core, plane),
                        ).wait_recv()
                return carry

            lax.fori_loop(1, n_chip // 2, wait_far, 0)

            def blank(step, carry):
                sums[(chip + 2 * step + 1) % n_chip] = jnp.zeros(sums.shape[1:], BF16)
                return carry

            lax.fori_loop(0, n_chip // 2, blank, 0)

    for k in range(chunks):
        acc = sums[0, k].astype(F32)
        for q in range(1, n_chip):
            acc += sums[q, k].astype(F32)
        out[k * width : (k + 1) * width, :] = acc.astype(BF16)

    def drain_blocks(step, carry):
        a_copy((me + step) % n_row).wait_send()
        return carry

    lax.fori_loop(1, n_row, drain_blocks, 0)

    def drain(n, carry):
        z, k = nearest(plane, n_col, n // chunks), n % chunks
        core_copy(z, k).wait_send()

        @pl.when(goes_right(z))
        def _():
            to_right(z, k).wait_send()

        @pl.when(goes_left(z))
        def _():
            to_left(z, k).wait_send()

        for j in range(chips_plane):
            target = z * chips_plane + j

            @pl.when(target != chip)
            def _():
                chip_copy(target, k).wait_send()

        return carry

    lax.fori_loop(0, steps, drain, 0)
    if share:

        @pl.when(is_end)
        def _():
            for q in range(pieces):
                kept_copy(q).wait_send()

            def drain_relay(e, carry):
                far, z, k, q = decode(e)
                for j in range(chips_plane):
                    target = z * chips_plane + j

                    @pl.when((target != chip) | (target % 2 != chip % 2))
                    def _():
                        relay_copy(far, j, k, q, target).wait_send()

                return carry

            lax.fori_loop(0, begin(chunks), drain_relay, 0)

        @pl.when(is_helper)
        def _():
            def drain_far(e, carry):
                far, z, k, q = decode(e)
                far_core_copy(far, k, q).wait_send()
                far_copy(far, k, q).wait_send()
                return carry

            lax.fori_loop(0, begin(chunks), drain_far, 0)


def body(integrals, coeffs, mask, offsets, atom_of_slot):
    n_row = lax.axis_size("row")
    n_col = lax.axis_size("col")
    me = lax.axis_index("row")
    plane = lax.axis_index("col")
    per_dev, atom_w, row_width = integrals.shape
    rows, cols = coeffs.shape
    cap = max(2, -(-per_dev // n_row))
    slots = n_row * cap
    block = cols * n_col // n_row
    chunks = max(1, min(4, block // 128))
    width = block // chunks
    per_plane = n_row // n_col

    holders = atom_of_slot.reshape(n_row, per_dev)
    slot = jnp.arange(per_dev, dtype=jnp.int32)
    mine = lax.dynamic_slice_in_dim(atom_of_slot, me * per_dev, per_dev)
    owner = mine // per_dev
    before = (owner[None, :] == owner[:, None]) & (slot[None, :] < slot[:, None])
    position = owner * cap + jnp.sum(before.astype(jnp.int32), axis=1)
    order = jnp.sum(
        jnp.where(jnp.arange(slots, dtype=jnp.int32)[:, None] == position[None, :], slot[None, :], 0), axis=1
    )
    is_mine = holders // per_dev == me
    earlier = is_mine[:, None, :] & (slot[None, None, :] < slot[None, :, None])
    arrival = jnp.sum(earlier.astype(jnp.int32), axis=2)
    place = (jnp.arange(n_row, dtype=jnp.int32)[:, None] * cap + arrival).reshape(-1)
    pick = jnp.sum(
        jnp.where((me * per_dev + slot)[:, None] == atom_of_slot[None, :], place[None, :], 0), axis=1
    )
    bounds = lax.dynamic_slice_in_dim(offsets, me * per_dev, per_dev + 1)
    lengths = bounds[1:] - bounds[:-1]
    significant = lax.dynamic_slice(mask, (me * per_dev, plane), (per_dev, 1))[:, 0]
    meta = jnp.concatenate([order, pick, lengths, significant])

    packed = rows * 3 // 4
    dma = pltpu.SemaphoreType.DMA
    n_chip = n_row // 2
    pair_width = per_plane * width
    n_far = max(1, n_col - 2)
    far_shape = (n_far, chunks, chunks, per_plane // 2, width, row_width // chunks)
    return pl.pallas_call(
        functools.partial(kernel, n_row, n_col, cap, chunks, width),
        out_shape=jax.ShapeDtypeStruct((block, row_width), BF16),
        in_specs=[pl.BlockSpec(memory_space=pltpu.SMEM)] + [pl.BlockSpec(memory_space=pltpu.VMEM)] * 2,
        out_specs=pl.BlockSpec(memory_space=pltpu.VMEM),
        scratch_shapes=[
            pltpu.VMEM((n_row, cap, atom_w, row_width), BF16),
            pltpu.VMEM((n_row, cap, atom_w, row_width), BF16),
            pltpu.VMEM((packed, row_width), BF16),
            pltpu.VMEM((n_col, chunks, packed, pair_width), BF16),
            pltpu.VMEM((n_chip, chunks, width, row_width), BF16),
            pltpu.VMEM((n_col, chunks, per_plane // 2, width, row_width), BF16),
            pltpu.VMEM((n_col, chunks, per_plane // 2, width, row_width), BF16),
            pltpu.VMEM((n_chip, chunks, width, row_width), BF16),
            pltpu.VMEM((packed, row_width), BF16),
            pltpu.VMEM(far_shape, BF16),
            pltpu.VMEM(far_shape, BF16),
            pltpu.VMEM(far_shape, BF16),
            pltpu.VMEM(far_shape, BF16),
            pltpu.VMEM(far_shape, BF16),
            dma((n_row,)),
            dma((n_row,)),
            dma((n_col, chunks)),
            dma((n_col, chunks)),
            dma((n_col, chunks)),
            dma((n_col, chunks)),
            dma((n_col, chunks)),
            dma((n_chip, chunks)),
            dma((n_chip, chunks)),
            dma((chunks,)),
            dma((chunks,)),
            dma((n_far, chunks, chunks)),
            dma((n_far, chunks, chunks)),
            dma((n_far, chunks, chunks)),
            dma((n_far, chunks, chunks)),
            dma((n_far, chunks, chunks, per_plane // 2)),
            dma((n_chip, chunks, chunks)),
            dma((n_far, chunks, chunks, per_plane // 2)),
        ],
        compiler_params=pltpu.CompilerParams(
            collective_id=0, has_side_effects=True, vmem_limit_bytes=62 << 20
        ),
    )(meta, integrals, coeffs)


def solution(mesh):
    in_specs = (P("row", None, "col"), P("row", "col"), P(), P(), P())
    out_specs = P("row", "col")
    return jax.shard_map(body, mesh=mesh, in_specs=in_specs, out_specs=out_specs, check_vma=False)
```

profile of v0, /device:TPU:6, one launch (start us, length us, event | category | flops | bytes accessed | tf_op | source)
XLA Modules:
  0.0 142.0 jit_solution(8894446887548166074)
XLA Ops:
  0.0 0.0 copy-start
  0.0 0.8 dynamic_slice.10
  0.8 0.1 slice_subtract_fusion
  0.8 0.0 copy-done
  0.8 0.1 dynamic-slice_bitcast_fusion
  0.9 0.8 and_select_fusion
  1.7 0.2 convert_reduce_fusion.1
  1.9 0.8 multiply_add_fusion
  2.6 0.1 select_reduce_fusion.1
  2.8 0.7 fusion.1
  3.5 0.1 and.36
  3.5 0.7 broadcast_divide_fusion
  4.2 0.1 div.21
  4.4 0.2 convert_reduce_fusion
  4.6 0.1 broadcast_add_fusion
  4.6 0.1 add.50
  4.7 0.9 select_reduce_fusion
  5.6 0.7 pad_add_fusion.meta
  6.2 133.5 %shard_map.55 = bf16[512,1024]{1,0:T(8,128)(2,1)} custom-call(s32[160]{0:T(256)} %pad_add_fusion.meta, bf16[40,32,1024]{2,1,0:T(8,128)(2,1)} %integrals.1, bf16[1280,1024]{1,0:T(8,128)(2,1)} %coeffs.1), custom_call_target="tpu_custom_call" | custom-call | tf_op jit(solution)/shard_map/pallas_call | solution.py:499
  139.7 2.3 %copy.7 = bf16[512,1024]{1,0:T(8,128)(2,1)} copy(bf16[512,1024]{1,0:T(8,128)(2,1)} %shard_map.55) | data formatting | bytes 2097152
  (4 shorter events, 0.0 us)
Async XLA Ops:
  0.0 0.8 copy-start
where the time goes:
time: 142 us
  Pallas kernels  133 us (94%)
  other arithmetic  5.12 us (4%)
  local copies, waits for them, and re-layouts  3.35 us (2%)
    pallas_call x1, Pallas kernels, body(): pl.pallas_call(functools.partial(kernel, n_row, n_col, cap, chunks, width...  133 us

commit v1 on v0

v1 whole, which is shorter than its diff:
```python
import functools

import jax
import jax.numpy as jnp
from jax import lax
from jax.experimental import pallas as pl
from jax.experimental.pallas import tpu as pltpu
from jax.sharding import PartitionSpec as P

MESH = pl.DeviceIdType.MESH
F32 = jnp.float32
BF16 = jnp.bfloat16
LANES = 128
EARLY = 2
PIECES = 4
HALVES = 2
JOIN = 2
LAG = 4
PASS_LAG = 2


def remote(src, dst, send, recv, device):
    return pltpu.make_async_remote_copy(
        src_ref=src, dst_ref=dst, send_sem=send, recv_sem=recv, device_id=device, device_id_type=MESH
    )


def nearest(me, n, s):
    m = jnp.minimum(me, n - 1 - me)
    step = (s + 1) // 2
    near = jnp.where(s % 2 == 1, me - step, me + step)
    far = jnp.where(me <= n - 1 - me, s, n - 1 - s)
    return jnp.where(s <= 2 * m, near, far)


def kernel(n_row, n_col, cap, n_chunk, *refs):
    meta, offsets, weight, integrals, coeffs, out = refs[:6]
    asend, arecv = refs[6 : 6 + PIECES], refs[6 + PIECES : 6 + 2 * PIECES]
    (
        kept, kept_end, gathered, work, core_in, work_far, core_far, pair, sums,
        a_ss, a_rs, r_ss, l_ss, g_rs, c_ss, c_rs, d_ss, d_rs, p_ss, p_rs, t_ss, t_rs, f_ss, f_rs, k_ss, k_rs,
    ) = refs[6 + 2 * PIECES :]
    me = lax.axis_index("row")
    plane = lax.axis_index("col")
    core = me % 2
    chip = me // 2
    n_chip = n_row // 2
    partner = me + 1 - 2 * core
    buddy = chip + 1 - 2 * (chip % 2)
    per_dev, atom_w, row_width = integrals.shape
    half = atom_w // 2
    pairs = per_dev // 2
    packed = 3 * half
    slots = n_row * cap
    per_plane = n_row // n_col
    chips_plane = per_plane // 2
    n_kb = n_chunk // per_plane
    piece = row_width // PIECES
    half_width = row_width // HALVES
    per_half = PIECES // HALVES
    n_far = n_col - 2
    inner = n_col - 2
    has_left = plane > 0
    has_right = plane < n_col - 1
    is_end = (plane == 0) | (plane == n_col - 1)
    is_helper = (plane == 1) | (plane == n_col - 2)
    low_half = plane <= n_col - 1 - plane
    near_end = jnp.where(low_half, 0, n_col - 1)
    far_end = n_col - 1 - near_end
    helper_plane = jnp.where(low_half, 1, n_col - 2)

    barrier = pltpu.get_barrier_semaphore()
    for other in range(1, n_row):
        pl.semaphore_signal(barrier, inc=1, device_id=((me + other) % n_row, plane), device_id_type=MESH)

    @pl.when(has_left)
    def _():
        pl.semaphore_signal(barrier, inc=1, device_id=(me, plane - 1), device_id_type=MESH)

    @pl.when(has_right)
    def _():
        pl.semaphore_signal(barrier, inc=1, device_id=(me, plane + 1), device_id_type=MESH)

    def selection(p, weighted):
        s = lax.broadcasted_iota(jnp.int32, (packed, 2 * atom_w), 0)
        t = lax.broadcasted_iota(jnp.int32, (packed, 2 * atom_w), 1)
        first = me * per_dev + 2 * p
        extra = offsets[first + 1] - offsets[first] - half
        source = jnp.where(
            s < half, s, jnp.where(s < 2 * half, s + half, jnp.where(s - 2 * half < extra, s - half, s + half - extra))
        )
        hit = source == t
        if weighted:
            sig = jnp.where(t < atom_w, weight[first], weight[first + 1])
            hit = hit & (sig > 0)
        return jnp.where(hit, 1.0, 0.0).astype(BF16)

    def column(n):
        return ((n % per_plane) * n_kb + n // per_plane) * LANES

    def pack_coeffs(chunks):
        def pack(p, carry):
            at = pl.ds(pl.multiple_of(p * packed, 16), packed)
            rows = pl.ds(pl.multiple_of(p * 2 * atom_w, 2 * atom_w), 2 * atom_w)
            pick = selection(p, False)
            live = jnp.concatenate([coeffs[rows, column(n) : column(n) + LANES] for n in chunks], axis=1)
            live = jnp.dot(pick, live, preferred_element_type=F32).astype(BF16)
            for i, n in enumerate(chunks):
                gathered[plane, n, at, :] = live[:, i * LANES : (i + 1) * LANES]
            return carry

        lax.fori_loop(0, pairs, pack, 0, unroll=4)

    def to_right(z, n):
        return remote(gathered.at[z, n], gathered.at[z, n], r_ss.at[z, n], g_rs.at[z, n], (me, plane + 1))

    def to_left(z, n):
        return remote(gathered.at[z, n], gathered.at[z, n], l_ss.at[z, n], g_rs.at[z, n], (me, plane - 1))

    def goes_right(z):
        return (z <= plane) & has_right & ((plane != n_col - 2) | (z == plane))

    def goes_left(z):
        return (z >= plane) & has_left & ((plane != 1) | (z == plane))

    def forward(z, n):
        @pl.when(goes_right(z))
        def _():
            to_right(z, n).start()

        @pl.when(goes_left(z))
        def _():
            to_left(z, n).start()

    early = min(EARLY, n_chunk)
    pack_coeffs(range(early))
    pl.semaphore_wait(barrier, n_row - 1 + has_left.astype(jnp.int32) + has_right.astype(jnp.int32))
    for n in range(early):
        forward(plane, n)

    def a_copy(q, owner):
        return remote(asend[q].at[owner], arecv[q].at[me], a_ss.at[q, owner], a_rs.at[q, me], (owner, plane))

    for q in range(PIECES):
        lanes = slice(q * piece, (q + 1) * piece)

        def place(step, carry):
            owner = (me + step) % n_row

            @pl.when(step > 0)
            def _():
                for c in range(cap):
                    asend[q][owner, c] = integrals[meta[owner * cap + c], :, lanes]
                a_copy(q, owner).start()

            @pl.when(step == 0)
            def _():
                for c in range(cap):
                    arecv[q][me, c] = integrals[meta[me * cap + c], :, lanes]

            return carry

        lax.fori_loop(0, n_row, place, 0)

    if early < n_chunk:
        pack_coeffs(range(early, n_chunk))

        @pl.when(jnp.logical_not(is_end))
        def _():
            for n in range(early, n_chunk):
                forward(plane, n)

    def kept_copy(q):
        lanes, there = pl.ds(q * piece, piece), pl.ds(q % per_half * piece, piece)
        return remote(
            kept.at[:, lanes], kept_end.at[q // per_half, :, there], k_ss.at[q], k_rs.at[q], (me, helper_plane)
        )

    for q in range(PIECES):
        lanes = slice(q * piece, (q + 1) * piece)

        def wait_blocks(step, carry):
            source = (me + step) % n_row
            remote(
                asend[q].at[source], arecv[q].at[source], a_ss.at[q, source], a_rs.at[q, source], (source, plane)
            ).wait_recv()
            return carry

        lax.fori_loop(1, n_row, wait_blocks, 0)

        def pack_kept(p, carry):
            first, second = meta[slots + 2 * p], meta[slots + 2 * p + 1]
            rows = jnp.concatenate(
                [arecv[q][first // cap, first % cap], arecv[q][second // cap, second % cap]], axis=0
            )
            live = jnp.dot(selection(p, True), rows, preferred_element_type=F32).astype(BF16)
            kept[pl.ds(pl.multiple_of(p * packed, 16), packed), lanes] = live
            return carry

        lax.fori_loop(0, pairs, pack_kept, 0, unroll=4)

        @pl.when(is_end)
        def _():
            kept_copy(q).start()

    def kept_copy_in(h, i):
        q, there = h * per_half + i, pl.ds(i * piece, piece)
        return remote(
            kept.at[:, there], kept_end.at[h, :, there], k_ss.at[q], k_rs.at[q], (me, helper_plane)
        )

    @pl.when(is_end)
    def _():
        for n in range(early, n_chunk):
            forward(plane, n)

    def arrive(z, n):
        to_right(z, n).wait_recv()
        forward(z, n)

    @pl.when(jnp.logical_not(is_end))
    def _():
        for n in range(early):
            arrive(near_end, n)

    inside = inner * (n_chunk // 2)
    per_pass = (n_far - 1) * (n_chunk // 2)
    one = inside + per_pass
    two = one + early // 2
    three = two + (HALVES - 1) * per_pass
    group = 2 + HALVES
    steps = jnp.where(is_end, n_chunk, three + group * n_chunk)
    beside = jnp.where(low_half, 1, n_col - 2)

    def far_plane(f):
        return jnp.where(low_half, f + 2, n_col - 3 - f)

    def decode(s):
        first = s < inside
        last = s >= three
        near_wide = (s >= one) & (s < two)
        far_wide = jnp.logical_not(first | last | near_wide)
        v = jnp.where(s < one, s - inside, s - two + per_pass)
        u = s - three
        m, r = u // group + 1, u % group
        near = last & (r == 0)
        far_single = last & (r > 0) & (r <= HALVES)
        far = (far_wide | far_single) & jnp.logical_not(is_end)
        z = jnp.where(
            first, 1 + nearest(plane - 1, inner, s % inner), jnp.where(near_wide | near, near_end, far_end)
        )
        n = jnp.where(
            first,
            s // inner * 2,
            jnp.where(near_wide, (s - one) * 2, jnp.where(far_wide, v % (n_chunk // 2) * 2, jnp.where(near, m, m - 1))),
        )
        f = jnp.where(far_wide, v % per_pass // (n_chunk // 2), n_far - 1)
        h = jnp.where(far_wide, v // per_pass, r - 1)
        z = jnp.where(far, far_plane(f), z)
        late = last & (n < n_chunk) & (jnp.logical_not(near) | (n >= early))
        valid = first | near_wide | (far_wide & is_helper) | (late & (is_helper | jnp.logical_not(far_single)))
        comes = (first & (z != plane)) | (late & (r <= 1))
        z = jnp.where(is_end, jnp.where(s % 2 == 0, plane, beside), z)
        n = jnp.where(is_end, s // 2 * 2, n)
        comes = jnp.where(is_end, s % 2 == 1, comes)
        wide = jnp.logical_not(last) | is_end
        running = (s >= 0) & (s < steps)
        valid = (valid | is_end) & running
        n = jnp.clip(n, 0, n_chunk - 1)
        h = jnp.clip(h, 0, HALVES - 1)
        return valid & jnp.logical_not(far), valid & far, comes & running, wide, z, n, f, h

    def mine(wide, n):
        return wide | (n % 2 == core), jnp.where(wide, n + core, n)

    def other(wide, n):
        return wide | (n % 2 != core), jnp.where(wide, n + 1 - core, n)

    def core_copy(z, n):
        return remote(work.at[z, n], core_in.at[z, n // 2], c_ss.at[z, n], c_rs.at[z, n // 2], (partner, plane))

    def far_core_copy(f, n, h):
        return remote(
            work_far.at[f, n, h], core_far.at[f, n // 2, h], d_ss.at[f, n, h], d_rs.at[f, n // 2, h], (partner, plane)
        )

    def far_copy(f, z, n, h, to):
        lanes = pl.ds(pl.multiple_of(h * half_width, LANES), half_width)
        return remote(work_far.at[f, n, h], work.at[z, n, :, lanes], f_ss.at[f, n, h], f_rs.at[f, n, h], (me, to))

    def target(z, n):
        return z * chips_plane + (n % per_plane) // 2

    def half_lanes(h):
        return pl.ds(pl.multiple_of(h * half_width, LANES), half_width)

    def pair_copy(z, n, h):
        return remote(
            work.at[z, n, :, half_lanes(h)], pair.at[z, n // 2, :, half_lanes(h)], p_ss.at[z, n, h],
            p_rs.at[z, n // 2, h], (2 * buddy + core, plane),
        )

    def target_copy(z, n, h):
        return remote(
            work.at[z, n, :, half_lanes(h)], sums.at[chip // 2, n // per_plane, :, half_lanes(h)], t_ss.at[z, n, h],
            t_rs.at[chip // 2, n // per_plane, h], (2 * target(z, n) + core, plane),
        )

    def sends_pair(z, n):
        return target(z, n) % 2 != chip % 2

    def sends_sum(z, n):
        return (target(z, n) % 2 == chip % 2) & (target(z, n) != chip)

    def multiply(lhs, rhs):
        return lax.dot_general(lhs, rhs, (((0,), (0,)), ((), ())), preferred_element_type=F32).astype(BF16)

    def add(x, y):
        return (x.astype(F32) + y.astype(F32)).astype(BF16)

    def compute(s):
        own, far, comes, wide, z, n, f, h = decode(s)

        @pl.when(comes)
        def _():
            arrive(z, n)

            @pl.when(wide)
            def _():
                arrive(z, n + 1)

        def both():
            return jnp.concatenate([gathered[z, n], gathered[z, n + 1]], axis=1)

        @pl.when(own & wide)
        def _():
            part = multiply(both(), kept[...])
            work[z, n] = part[:LANES]
            work[z, n + 1] = part[LANES:]

        @pl.when(own & jnp.logical_not(wide))
        def _():
            work[z, n] = multiply(gathered[z, n], kept[...])

        @pl.when(far & wide)
        def _():
            @pl.when((f == 0) & (n == 0))
            def _():
                for i in range(per_half):
                    kept_copy_in(h, i).wait_recv()

            part = multiply(both(), kept_end[h])
            work_far[f, n, h] = part[:LANES]
            work_far[f, n + 1, h] = part[LANES:]

        @pl.when(far & jnp.logical_not(wide))
        def _():
            work_far[f, n, h] = multiply(gathered[z, n], kept_end[h])

        there, n_other = other(wide, n)

        @pl.when(own & there)
        def _():
            core_copy(z, n_other).start()

        @pl.when(far & there)
        def _():
            far_core_copy(f, n_other, h).start()

    def join_cores(s):
        own, far, comes, wide, z, n, f, h = decode(s)
        here, n = mine(wide, n)

        @pl.when(own & here)
        def _():
            core_copy(z, n).wait_recv()
            work[z, n] = add(work[z, n], core_in[z, n // 2])

            @pl.when(sends_pair(z, n))
            def _():
                for i in range(HALVES):
                    pair_copy(z, n, i).start()

        @pl.when(far & here)
        def _():
            far_core_copy(f, n, h).wait_recv()
            work_far[f, n, h] = add(work_far[f, n, h], core_far[f, n // 2, h])
            far_copy(f, z, n, h, near_end).start()

    def join_chips(s, carry):
        own, far, comes, wide, z, n, f, h = decode(s)
        here, n = mine(wide, n)

        @pl.when(own & here & sends_sum(z, n))
        def _():
            for i in range(HALVES):
                pair_copy(z, n, i).wait_recv()
            work[z, n] = add(work[z, n], pair[z, n // 2])
            for i in range(HALVES):
                target_copy(z, n, i).start()

        return carry

    def joined(s):
        return jnp.clip(jnp.minimum(2 * (s - three + 1), s - LAG), 0, steps)

    def step_body(s, carry):
        compute(s)
        join_cores(s - JOIN)
        lax.fori_loop(joined(s - 1), joined(s), join_chips, 0)
        return carry

    lax.fori_loop(0, steps + JOIN, step_body, 0)
    lax.fori_loop(joined(steps + JOIN - 1), steps, join_chips, 0)

    n_pass = n_far * n_chunk * HALVES

    def passed(e):
        v = e % ((n_far - 1) * n_chunk)
        w = e - (n_far - 1) * n_chunk * HALVES
        f = jnp.where(w < 0, v // n_chunk, n_far - 1)
        n = jnp.where(w < 0, v % n_chunk, w // HALVES)
        h = jnp.where(w < 0, e // ((n_far - 1) * n_chunk), w % HALVES)
        return f, far_plane(f), n, h

    @pl.when(is_end)
    def _():
        def pass_on(e, carry):
            @pl.when(e < n_pass)
            def _():
                f, z, n, h = passed(e)

                @pl.when(n % 2 == core)
                def _():
                    far_copy(f, z, n, h, plane).wait_recv()

                    @pl.when(sends_pair(z, n))
                    def _():
                        pair_copy(z, n, h).start()

            @pl.when(e >= PASS_LAG)
            def _():
                f, z, n, h = passed(e - PASS_LAG)

                @pl.when((n % 2 == core) & sends_sum(z, n))
                def _():
                    pair_copy(z, n, h).wait_recv()
                    lanes = half_lanes(h)
                    work[z, n, :, lanes] = add(work[z, n, :, lanes], pair[z, n // 2, :, lanes])
                    target_copy(z, n, h).start()

            return carry

        lax.fori_loop(0, n_pass + PASS_LAG, pass_on, 0)

    own_z, own_b = me // per_plane, me % per_plane
    for kb in range(n_kb):
        n = kb * per_plane + own_b
        for h in range(HALVES):
            pair_copy(own_z, n, h).wait_recv()
        total = work[own_z, n].astype(F32) + pair[own_z, n // 2].astype(F32)
        for step in range(1, n_chip // 2):
            source = (chip // 2 + step) % (n_chip // 2)
            for h in range(HALVES):
                remote(
                    work.at[own_z, n, :, half_lanes(h)], sums.at[source, kb, :, half_lanes(h)], t_ss.at[own_z, n, h],
                    t_rs.at[source, kb, h], (2 * (2 * source + chip % 2) + core, plane),
                ).wait_recv()
            total += sums[source, kb].astype(F32)
        out[kb * LANES : (kb + 1) * LANES, :] = total.astype(BF16)

    def drain_blocks(step, carry):
        for q in range(PIECES):
            a_copy(q, (me + step) % n_row).wait_send()
        return carry

    lax.fori_loop(1, n_row, drain_blocks, 0)

    def drain_sums(z, n, h):
        @pl.when(sends_pair(z, n))
        def _():
            pair_copy(z, n, h).wait_send()

        @pl.when(sends_sum(z, n))
        def _():
            target_copy(z, n, h).wait_send()

    def drain(s, carry):
        own, far, comes, wide, z, n, f, h = decode(s)
        here, n_mine = mine(wide, n)
        there, n_other = other(wide, n)

        @pl.when(own & there)
        def _():
            core_copy(z, n_other).wait_send()

        @pl.when(far & there)
        def _():
            far_core_copy(f, n_other, h).wait_send()

        @pl.when(far & here)
        def _():
            far_copy(f, z, n_mine, h, near_end).wait_send()

        @pl.when(own & here)
        def _():
            for i in range(HALVES):
                drain_sums(z, n_mine, i)

        return carry

    lax.fori_loop(0, steps, drain, 0)

    def drain_gathered(e, carry):
        z, n = e // n_chunk, e % n_chunk

        @pl.when(goes_right(z))
        def _():
            to_right(z, n).wait_send()

        @pl.when(goes_left(z))
        def _():
            to_left(z, n).wait_send()

        return carry

    lax.fori_loop(0, n_col * n_chunk, drain_gathered, 0)

    @pl.when(is_end)
    def _():
        for q in range(PIECES):
            kept_copy(q).wait_send()

        def drain_pass(e, carry):
            f, z, n, h = passed(e)

            @pl.when(n % 2 == core)
            def _():
                drain_sums(z, n, h)

            return carry

        lax.fori_loop(0, n_pass, drain_pass, 0)


def body(integrals, coeffs, mask, offsets, atom_of_slot):
    n_row = lax.axis_size("row")
    n_col = lax.axis_size("col")
    me = lax.axis_index("row")
    per_dev, atom_w, row_width = integrals.shape
    rows, cols = coeffs.shape
    cap = max(2, -(-per_dev // n_row))
    slots = n_row * cap
    n_atom = atom_of_slot.shape[0]
    block = cols * n_col // n_row
    n_chunk = cols // LANES
    n_kb = block // LANES

    slot = jnp.arange(n_atom, dtype=jnp.int32)
    owner = atom_of_slot // per_dev
    holder = slot // per_dev
    flow = holder * n_row + owner
    rank = jnp.sum(((flow[None, :] == flow[:, None]) & (slot[None, :] < slot[:, None])).astype(jnp.int32), axis=1)
    goes = jnp.where(holder == me, owner * cap + rank, -1)
    comes = atom_of_slot - me * per_dev + slots
    entry = jnp.arange(slots + per_dev, dtype=jnp.int32)[:, None]
    meta = jnp.sum(
        jnp.where(
            entry < slots,
            jnp.where(goes[None, :] == entry, (slot - me * per_dev)[None, :], 0),
            jnp.where(comes[None, :] == entry, (holder * cap + rank)[None, :], 0),
        ),
        axis=1,
    )

    column = jnp.arange(n_col, dtype=jnp.int32)[None, :] == lax.axis_index("col")
    weight = jnp.sum(jnp.where(column, mask, 0), axis=1)

    packed = rows * 3 // 4
    dma = pltpu.SemaphoreType.DMA
    n_chip = n_row // 2
    n_far = n_col - 2
    narrow = row_width // HALVES
    moved = [pltpu.VMEM((n_row, cap, atom_w, row_width // PIECES), BF16)] * (2 * PIECES)
    smem = pl.BlockSpec(memory_space=pltpu.SMEM)
    vmem = pl.BlockSpec(memory_space=pltpu.VMEM)
    return pl.pallas_call(
        functools.partial(kernel, n_row, n_col, cap, n_chunk),
        out_shape=jax.ShapeDtypeStruct((block, row_width), BF16),
        in_specs=[smem, smem, smem, vmem, vmem],
        out_specs=vmem,
        scratch_shapes=moved
        + [
            pltpu.VMEM((packed, row_width), BF16),
            pltpu.VMEM((HALVES, packed, narrow), BF16),
            pltpu.VMEM((n_col, n_chunk, packed, LANES), BF16),
            pltpu.VMEM((n_col, n_chunk, LANES, row_width), BF16),
            pltpu.VMEM((n_col, n_chunk // 2, LANES, row_width), BF16),
            pltpu.VMEM((n_far, n_chunk, HALVES, LANES, narrow), BF16),
            pltpu.VMEM((n_far, n_chunk // 2, HALVES, LANES, narrow), BF16),
            pltpu.VMEM((n_col, n_chunk // 2, LANES, row_width), BF16),
            pltpu.VMEM((n_chip // 2, n_kb, LANES, row_width), BF16),
            dma((PIECES, n_row)),
            dma((PIECES, n_row)),
            dma((n_col, n_chunk)),
            dma((n_col, n_chunk)),
            dma((n_col, n_chunk)),
            dma((n_col, n_chunk)),
            dma((n_col, n_chunk // 2)),
            dma((n_far, n_chunk, HALVES)),
            dma((n_far, n_chunk // 2, HALVES)),
            dma((n_col, n_chunk, HALVES)),
            dma((n_col, n_chunk // 2, HALVES)),
            dma((n_col, n_chunk, HALVES)),
            dma((n_chip // 2, n_kb, HALVES)),
            dma((n_far, n_chunk, HALVES)),
            dma((n_far, n_chunk, HALVES)),
            dma((PIECES,)),
            dma((PIECES,)),
        ],
        compiler_params=pltpu.CompilerParams(
            collective_id=0, has_side_effects=True, vmem_limit_bytes=62 << 20
        ),
    )(meta, offsets, weight, integrals, coeffs)


def solution(mesh):
    in_specs = (P("row", None, "col"), P("row", "col"), P(), P(), P())
    out_specs = P("row", "col")
    return jax.shard_map(body, mesh=mesh, in_specs=in_specs, out_specs=out_specs, check_vma=False)
```

time: 142 us -> 132 us (0.930)
  the two profiles are of different devices: /device:TPU:6 before, /device:TPU:15 now
where the time goes in v1:
time: 132 us; the launch traced here: 131 us
  Pallas kernels  125 us (95%)
  other arithmetic  3.76 us (3%)
  local copies, waits for them, and re-layouts  2.26 us (2%)
    pallas_call x1, Pallas kernels, body(): pl.pallas_call(functools.partial(kernel, n_row, n_col, cap, n_chunk), out...  125 us

profile of v1, /device:TPU:15, one launch (start us, length us, event | category | flops | bytes accessed | tf_op | source)
XLA Modules:
  0.0 131.4 jit_solution(13389079972048720566)
XLA Ops:
  0.0 1.4 %select_reduce_fusion.1.refs_2_ = s32[320]{0:T(512)} fusion(s32[320,4]{0,1:T(4,128)} %param.7, pred[4]{0:T(512)(128)(4,1)S(1)} %iota_compare_fusion.3), kind=kLoop, calls=%fused_computation.6 | loop fusion | flops 2240 | bytes 6404 | tf_op jit(solution)/shard_map/reduce_sum | solution.py:577
  1.4 0.7 multiply_add_fusion.1
  2.1 0.2 convert_reduce_fusion
  2.3 0.7 add_select_fusion.2
  3.0 0.8 select_reduce_fusion.refs_0_
  3.8 125.4 %shard_map.55 = bf16[512,1024]{1,0:T(8,128)(2,1)} custom-call(s32[80]{0:T(128)} %select_reduce_fusion.refs_0_, s32[321]{0:T(512)} %refs_1_.1, s32[320]{0:T(512)} %select_reduce_fusion.1.refs_2_, bf16[40,32,1024]{2,1,0:T(8,128)(2,1)} %refs_3_.1, bf16[1280,1024]{1,0:T(8,128)(2,1)} %refs_4_.1), custom_call_target="tpu_custom_call" | custom-call | tf_op jit(solution)/shard_map/pallas_call | solution.py:587
  129.2 2.3 %copy.7 = bf16[512,1024]{1,0:T(8,128)(2,1)} copy(bf16[512,1024]{1,0:T(8,128)(2,1)} %shard_map.55) | data formatting | bytes 2097152
  (2 shorter events, 0.0 us)

commit v2 on v1

--- a/solution.py
+++ b/solution.py
@@ -34,7 +34,7 @@
 
 
 def kernel(n_row, n_col, cap, n_chunk, *refs):
-    meta, offsets, weight, integrals, coeffs, out = refs[:6]
+    meta, offsets, mask, integrals, coeffs, out = refs[:6]
     asend, arecv = refs[6 : 6 + PIECES], refs[6 + PIECES : 6 + 2 * PIECES]
     (
         kept, kept_end, gathered, work, core_in, work_far, core_far, pair, sums,
@@ -91,7 +91,7 @@
         )
         hit = source == t
         if weighted:
-            sig = jnp.where(t < atom_w, weight[first], weight[first + 1])
+            sig = jnp.where(t < atom_w, mask[plane, first], mask[plane, first + 1])
             hit = hit & (sig > 0)
         return jnp.where(hit, 1.0, 0.0).astype(BF16)
 
@@ -112,10 +112,10 @@
         lax.fori_loop(0, pairs, pack, 0, unroll=4)
 
     def to_right(z, n):
-        return remote(gathered.at[z, n], gathered.at[z, n], r_ss.at[z, n], g_rs.at[z, n], (me, plane + 1))
+        return remote(gathered.at[z, n], gathered.at[z, n], r_ss.at[z], g_rs.at[z, n], (me, plane + 1))
 
     def to_left(z, n):
-        return remote(gathered.at[z, n], gathered.at[z, n], l_ss.at[z, n], g_rs.at[z, n], (me, plane - 1))
+        return remote(gathered.at[z, n], gathered.at[z, n], l_ss.at[z], g_rs.at[z, n], (me, plane - 1))
 
     def goes_right(z):
         return (z <= plane) & has_right & ((plane != n_col - 2) | (z == plane))
@@ -277,16 +277,16 @@
         return wide | (n % 2 != core), jnp.where(wide, n + 1 - core, n)
 
     def core_copy(z, n):
-        return remote(work.at[z, n], core_in.at[z, n // 2], c_ss.at[z, n], c_rs.at[z, n // 2], (partner, plane))
+        return remote(work.at[z, n], core_in.at[z, n // 2], c_ss, c_rs.at[z, n // 2], (partner, plane))
 
     def far_core_copy(f, n, h):
         return remote(
-            work_far.at[f, n, h], core_far.at[f, n // 2, h], d_ss.at[f, n, h], d_rs.at[f, n // 2, h], (partner, plane)
+            work_far.at[f, n, h], core_far.at[f, n // 2, h], d_ss, d_rs.at[f, n // 2, h], (partner, plane)
         )
 
     def far_copy(f, z, n, h, to):
         lanes = pl.ds(pl.multiple_of(h * half_width, LANES), half_width)
-        return remote(work_far.at[f, n, h], work.at[z, n, :, lanes], f_ss.at[f, n, h], f_rs.at[f, n, h], (me, to))
+        return remote(work_far.at[f, n, h], work.at[z, n, :, lanes], f_ss, f_rs.at[f, n, h], (me, to))
 
     def target(z, n):
         return z * chips_plane + (n % per_plane) // 2
@@ -296,13 +296,13 @@
 
     def pair_copy(z, n, h):
         return remote(
-            work.at[z, n, :, half_lanes(h)], pair.at[z, n // 2, :, half_lanes(h)], p_ss.at[z, n, h],
+            work.at[z, n, :, half_lanes(h)], pair.at[z, n // 2, :, half_lanes(h)], p_ss,
             p_rs.at[z, n // 2, h], (2 * buddy + core, plane),
         )
 
     def target_copy(z, n, h):
         return remote(
-            work.at[z, n, :, half_lanes(h)], sums.at[chip // 2, n // per_plane, :, half_lanes(h)], t_ss.at[z, n, h],
+            work.at[z, n, :, half_lanes(h)], sums.at[chip // 2, n // per_plane, :, half_lanes(h)], t_ss,
             t_rs.at[chip // 2, n // per_plane, h], (2 * target(z, n) + core, plane),
         )
 
@@ -395,8 +395,8 @@
         def _():
             for i in range(HALVES):
                 pair_copy(z, n, i).wait_recv()
-            work[z, n] = add(work[z, n], pair[z, n // 2])
-            for i in range(HALVES):
+                lanes = pl.ds(i * half_width, half_width)
+                work[z, n, :, lanes] = add(work[z, n, :, lanes], pair[z, n // 2, :, lanes])
                 target_copy(z, n, i).start()
 
         return carry
@@ -463,7 +463,7 @@
             source = (chip // 2 + step) % (n_chip // 2)
             for h in range(HALVES):
                 remote(
-                    work.at[own_z, n, :, half_lanes(h)], sums.at[source, kb, :, half_lanes(h)], t_ss.at[own_z, n, h],
+                    work.at[own_z, n, :, half_lanes(h)], sums.at[source, kb, :, half_lanes(h)], t_ss,
                     t_rs.at[source, kb, h], (2 * (2 * source + chip % 2) + core, plane),
                 ).wait_recv()
             total += sums[source, kb].astype(F32)
@@ -476,71 +476,40 @@
 
     lax.fori_loop(1, n_row, drain_blocks, 0)
 
-    def drain_sums(z, n, h):
-        @pl.when(sends_pair(z, n))
-        def _():
-            pair_copy(z, n, h).wait_send()
-
-        @pl.when(sends_sum(z, n))
-        def _():
-            target_copy(z, n, h).wait_send()
-
-    def drain(s, carry):
-        own, far, comes, wide, z, n, f, h = decode(s)
-        here, n_mine = mine(wide, n)
-        there, n_other = other(wide, n)
-
-        @pl.when(own & there)
-        def _():
-            core_copy(z, n_other).wait_send()
-
-        @pl.when(far & there)
-        def _():
-            far_core_copy(f, n_other, h).wait_send()
-
-        @pl.when(far & here)
-        def _():
-            far_copy(f, z, n_mine, h, near_end).wait_send()
-
-        @pl.when(own & here)
-        def _():
-            for i in range(HALVES):
-                drain_sums(z, n_mine, i)
-
-        return carry
-
-    lax.fori_loop(0, steps, drain, 0)
-
-    def drain_gathered(e, carry):
-        z, n = e // n_chunk, e % n_chunk
-
-        @pl.when(goes_right(z))
-        def _():
-            to_right(z, n).wait_send()
-
-        @pl.when(goes_left(z))
-        def _():
-            to_left(z, n).wait_send()
-
-        return carry
-
-    lax.fori_loop(0, n_col * n_chunk, drain_gathered, 0)
+    def sent(ref, sem):
+        remote(ref, ref, sem, sem, (partner, plane)).wait_send()
+
+    sent(pair.at[: n_col // 2], p_ss)
+    if n_chip > 2:
+        sent(sums.at[: n_chip // 2 - 1], t_ss)
 
     @pl.when(is_end)
     def _():
+        sent(core_in.at[:2], c_ss)
         for q in range(PIECES):
             kept_copy(q).wait_send()
 
-        def drain_pass(e, carry):
-            f, z, n, h = passed(e)
-
-            @pl.when(n % 2 == core)
-            def _():
-                drain_sums(z, n, h)
-
-            return carry
-
-        lax.fori_loop(0, n_pass, drain_pass, 0)
+    @pl.when(jnp.logical_not(is_end))
+    def _():
+        sent(core_in, c_ss)
+
+    @pl.when(is_helper)
+    def _():
+        sent(core_far, d_ss)
+        sent(core_far, f_ss)
+
+    def drain_gathered(z, carry):
+        @pl.when(goes_right(z))
+        def _():
+            sent(gathered.at[z], r_ss.at[z])
+
+        @pl.when(goes_left(z))
+        def _():
+            sent(gathered.at[z], l_ss.at[z])
+
+        return carry
+
+    lax.fori_loop(0, n_col, drain_gathered, 0)
 
 
 def body(integrals, coeffs, mask, offsets, atom_of_slot):
@@ -551,10 +520,11 @@
     rows, cols = coeffs.shape
     cap = max(2, -(-per_dev // n_row))
     slots = n_row * cap
-    n_atom = atom_of_slot.shape[0]
     block = cols * n_col // n_row
     n_chunk = cols // LANES
     n_kb = block // LANES
+
+    n_atom = atom_of_slot.shape[0]
 
     slot = jnp.arange(n_atom, dtype=jnp.int32)
     owner = atom_of_slot // per_dev
@@ -572,9 +542,6 @@
         ),
         axis=1,
     )
-
-    column = jnp.arange(n_col, dtype=jnp.int32)[None, :] == lax.axis_index("col")
-    weight = jnp.sum(jnp.where(column, mask, 0), axis=1)
 
     packed = rows * 3 // 4
     dma = pltpu.SemaphoreType.DMA
@@ -602,18 +569,18 @@
             pltpu.VMEM((n_chip // 2, n_kb, LANES, row_width), BF16),
             dma((PIECES, n_row)),
             dma((PIECES, n_row)),
+            dma((n_col,)),
+            dma((n_col,)),
             dma((n_col, n_chunk)),
-            dma((n_col, n_chunk)),
-            dma((n_col, n_chunk)),
-            dma((n_col, n_chunk)),
+            dma,
             dma((n_col, n_chunk // 2)),
-            dma((n_far, n_chunk, HALVES)),
+            dma,
             dma((n_far, n_chunk // 2, HALVES)),
-            dma((n_col, n_chunk, HALVES)),
+            dma,
             dma((n_col, n_chunk // 2, HALVES)),
-            dma((n_col, n_chunk, HALVES)),
+            dma,
             dma((n_chip // 2, n_kb, HALVES)),
-            dma((n_far, n_chunk, HALVES)),
+            dma,
             dma((n_far, n_chunk, HALVES)),
             dma((PIECES,)),
             dma((PIECES,)),
@@ -621,7 +588,7 @@
         compiler_params=pltpu.CompilerParams(
             collective_id=0, has_side_effects=True, vmem_limit_bytes=62 << 20
         ),
-    )(meta, offsets, weight, integrals, coeffs)
+    )(meta, offsets, mask.T, integrals, coeffs)
 
 
 def solution(mesh):

time: 132 us -> 122 us (0.924)
  the two profiles are of different devices: /device:TPU:15 before, /device:TPU:25 now
where the time goes in v2:
time: 122 us; the launch traced here: 121 us
  Pallas kernels  117 us (96%)
  other arithmetic  2.32 us (2%)
  local copies, waits for them, and re-layouts  2.26 us (2%)
    pallas_call x1, Pallas kernels, body(): pl.pallas_call(functools.partial(kernel, n_row, n_col, cap, n_chunk), out...  117 us

profile of v2, /device:TPU:25, one launch (start us, length us, event | category | flops | bytes accessed | tf_op | source)
XLA Modules:
  0.0 121.5 jit_solution(6409481201170515962)
XLA Ops:
  0.0 0.7 multiply_add_fusion.1
  0.7 0.2 convert_reduce_fusion
  0.9 0.7 add_select_fusion.2
  1.6 0.7 select_reduce_fusion.refs_0_
  2.3 116.9 %shard_map.55 = bf16[512,1024]{1,0:T(8,128)(2,1)} custom-call(s32[80]{0:T(128)} %select_reduce_fusion.refs_0_, s32[321]{0:T(512)} %refs_1_.1, s32[4,320]{1,0:T(4,128)} %bitcast.1, bf16[40,32,1024]{2,1,0:T(8,128)(2,1)} %refs_3_.1, bf16[1280,1024]{1,0:T(8,128)(2,1)} %refs_4_.1), custom_call_target="tpu_custom_call" | custom-call | tf_op jit(solution)/shard_map/pallas_call | solution.py:554
  119.2 2.3 %copy.7 = bf16[512,1024]{1,0:T(8,128)(2,1)} copy(bf16[512,1024]{1,0:T(8,128)(2,1)} %shard_map.55) | data formatting | bytes 2097152
  (1 shorter events, 0.0 us)

commit v3 on v2

--- a/solution.py
+++ b/solution.py
@@ -14,6 +14,7 @@
 EARLY = 2
 PIECES = 4
 HALVES = 2
+PARTS = 1
 JOIN = 2
 LAG = 4
 PASS_LAG = 2
@@ -111,11 +112,14 @@
 
         lax.fori_loop(0, pairs, pack, 0, unroll=4)
 
-    def to_right(z, n):
-        return remote(gathered.at[z, n], gathered.at[z, n], r_ss.at[z], g_rs.at[z, n], (me, plane + 1))
-
-    def to_left(z, n):
-        return remote(gathered.at[z, n], gathered.at[z, n], l_ss.at[z], g_rs.at[z, n], (me, plane - 1))
+    def part_of(z, n, i):
+        return gathered.at[z, n, pl.ds(i * (pairs * packed // PARTS), pairs * packed // PARTS)]
+
+    def to_right(z, n, i):
+        return remote(part_of(z, n, i), part_of(z, n, i), r_ss.at[z], g_rs.at[z, n, i], (me, plane + 1))
+
+    def to_left(z, n, i):
+        return remote(part_of(z, n, i), part_of(z, n, i), l_ss.at[z], g_rs.at[z, n, i], (me, plane - 1))
 
     def goes_right(z):
         return (z <= plane) & has_right & ((plane != n_col - 2) | (z == plane))
@@ -123,14 +127,16 @@
     def goes_left(z):
         return (z >= plane) & has_left & ((plane != 1) | (z == plane))
 
-    def forward(z, n):
+    def forward(z, n, parts=range(PARTS)):
         @pl.when(goes_right(z))
         def _():
-            to_right(z, n).start()
+            for i in parts:
+                to_right(z, n, i).start()
 
         @pl.when(goes_left(z))
         def _():
-            to_left(z, n).start()
+            for i in parts:
+                to_left(z, n, i).start()
 
     early = min(EARLY, n_chunk)
     pack_coeffs(range(early))
@@ -215,8 +221,9 @@
             forward(plane, n)
 
     def arrive(z, n):
-        to_right(z, n).wait_recv()
-        forward(z, n)
+        for i in range(PARTS):
+            to_right(z, n, i).wait_recv()
+            forward(z, n, [i])
 
     @pl.when(jnp.logical_not(is_end))
     def _():
@@ -235,14 +242,23 @@
     def far_plane(f):
         return jnp.where(low_half, f + 2, n_col - 3 - f)
 
-    def decode(s):
+    def reordered(s):
+        if n_far != 2:
+            return s
+        own, far = inside - inner, per_pass - 1
+        later = jnp.where(s < own + far + inner, s - far, s)
+        return jnp.where(s < own, s, jnp.where(s < own + far, s + inner, later))
+
+    def decode(at):
+        running = (at >= 0) & (at < steps)
+        s = jnp.where(is_end, at, reordered(at))
         first = s < inside
         last = s >= three
         near_wide = (s >= one) & (s < two)
         far_wide = jnp.logical_not(first | last | near_wide)
         v = jnp.where(s < one, s - inside, s - two + per_pass)
         u = s - three
-        m, r = u // group + 1, u % group
+        m, r = u // group, u % group
         near = last & (r == 0)
         far_single = last & (r > 0) & (r <= HALVES)
         far = (far_wide | far_single) & jnp.logical_not(is_end)
@@ -252,19 +268,18 @@
         n = jnp.where(
             first,
             s // inner * 2,
-            jnp.where(near_wide, (s - one) * 2, jnp.where(far_wide, v % (n_chunk // 2) * 2, jnp.where(near, m, m - 1))),
+            jnp.where(near_wide, (s - one) * 2, jnp.where(far_wide, v % (n_chunk // 2) * 2, jnp.where(near, m + early, m))),
         )
         f = jnp.where(far_wide, v % per_pass // (n_chunk // 2), n_far - 1)
         h = jnp.where(far_wide, v // per_pass, r - 1)
         z = jnp.where(far, far_plane(f), z)
-        late = last & (n < n_chunk) & (jnp.logical_not(near) | (n >= early))
+        late = last & (n < n_chunk)
         valid = first | near_wide | (far_wide & is_helper) | (late & (is_helper | jnp.logical_not(far_single)))
         comes = (first & (z != plane)) | (late & (r <= 1))
         z = jnp.where(is_end, jnp.where(s % 2 == 0, plane, beside), z)
         n = jnp.where(is_end, s // 2 * 2, n)
         comes = jnp.where(is_end, s % 2 == 1, comes)
         wide = jnp.logical_not(last) | is_end
-        running = (s >= 0) & (s < steps)
         valid = (valid | is_end) & running
         n = jnp.clip(n, 0, n_chunk - 1)
         h = jnp.clip(h, 0, HALVES - 1)
@@ -527,12 +542,13 @@
     n_atom = atom_of_slot.shape[0]
 
     slot = jnp.arange(n_atom, dtype=jnp.int32)
-    owner = atom_of_slot // per_dev
+    local = lax.optimization_barrier(atom_of_slot - me * per_dev)
+    owner = (local + me * per_dev) // per_dev
     holder = slot // per_dev
     flow = holder * n_row + owner
     rank = jnp.sum(((flow[None, :] == flow[:, None]) & (slot[None, :] < slot[:, None])).astype(jnp.int32), axis=1)
     goes = jnp.where(holder == me, owner * cap + rank, -1)
-    comes = atom_of_slot - me * per_dev + slots
+    comes = local + slots
     entry = jnp.arange(slots + per_dev, dtype=jnp.int32)[:, None]
     meta = jnp.sum(
         jnp.where(
@@ -571,7 +587,7 @@
             dma((PIECES, n_row)),
             dma((n_col,)),
             dma((n_col,)),
-            dma((n_col, n_chunk)),
+            dma((n_col, n_chunk, PARTS)),
             dma,
             dma((n_col, n_chunk // 2)),
             dma,

time: 122 us -> 121 us (level)
  no operation moved by 1% of the time
where the time goes in v3:
time: 121 us
  Pallas kernels  117 us (97%)
  local copies, waits for them, and re-layouts  2.26 us (2%)
  other arithmetic  1.64 us (1%)
    pallas_call x1, Pallas kernels, body(): pl.pallas_call(functools.partial(kernel, n_row, n_col, cap, n_chunk), out...  117 us

profile of v3, /device:TPU:25, one launch (start us, length us, event | category | flops | bytes accessed | tf_op | source)
XLA Modules:
  0.0 120.5 jit_solution(10871765507060782124)
XLA Ops:
  0.0 0.7 broadcast_subtract_fusion
  0.7 0.2 convert_reduce_fusion
  1.0 0.7 select_reduce_fusion.refs_0_
  1.7 116.6 %shard_map.55 = bf16[512,1024]{1,0:T(8,128)(2,1)} custom-call(s32[80]{0:T(128)} %select_reduce_fusion.refs_0_, s32[321]{0:T(512)} %refs_1_.1, s32[4,320]{1,0:T(4,128)} %bitcast.1, bf16[40,32,1024]{2,1,0:T(8,128)(2,1)} %refs_3_.1, bf16[1280,1024]{1,0:T(8,128)(2,1)} %refs_4_.1), custom_call_target="tpu_custom_call" | custom-call | tf_op jit(solution)/shard_map/pallas_call | solution.py:570
  118.3 2.3 %copy.7 = bf16[512,1024]{1,0:T(8,128)(2,1)} copy(bf16[512,1024]{1,0:T(8,128)(2,1)} %shard_map.55) | data formatting | bytes 2097152
  (3 shorter events, 0.0 us)

commit v4 on v3

--- a/solution.py
+++ b/solution.py
@@ -15,8 +15,8 @@
 PIECES = 4
 HALVES = 2
 PARTS = 1
-JOIN = 2
-LAG = 4
+JOIN = 1
+LAG = 3
 PASS_LAG = 2
 
 
@@ -235,7 +235,7 @@
     one = inside + per_pass
     two = one + early // 2
     three = two + (HALVES - 1) * per_pass
-    group = 2 + HALVES
+    group = 3
     steps = jnp.where(is_end, n_chunk, three + group * n_chunk)
     beside = jnp.where(low_half, 1, n_col - 2)
 
@@ -260,7 +260,7 @@
         u = s - three
         m, r = u // group, u % group
         near = last & (r == 0)
-        far_single = last & (r > 0) & (r <= HALVES)
+        far_single = last & (r == 1)
         far = (far_wide | far_single) & jnp.logical_not(is_end)
         z = jnp.where(
             first, 1 + nearest(plane - 1, inner, s % inner), jnp.where(near_wide | near, near_end, far_end)
@@ -370,7 +370,8 @@
 
         @pl.when(far & jnp.logical_not(wide))
         def _():
-            work_far[f, n, h] = multiply(gathered[z, n], kept_end[h])
+            for i in range(HALVES):
+                work_far[f, n, i] = multiply(gathered[z, n], kept_end[i])
 
         there, n_other = other(wide, n)
 
@@ -378,9 +379,19 @@
         def _():
             core_copy(z, n_other).start()
 
-        @pl.when(far & there)
+        @pl.when(far & there & wide)
         def _():
             far_core_copy(f, n_other, h).start()
+
+        @pl.when(far & there & jnp.logical_not(wide))
+        def _():
+            for i in range(HALVES):
+                far_core_copy(f, n_other, i).start()
+
+    def join_far(f, z, n, h):
+        far_core_copy(f, n, h).wait_recv()
+        work_far[f, n, h] = add(work_far[f, n, h], core_far[f, n // 2, h])
+        far_copy(f, z, n, h, near_end).start()
 
     def join_cores(s):
         own, far, comes, wide, z, n, f, h = decode(s)
@@ -396,11 +407,14 @@
                 for i in range(HALVES):
                     pair_copy(z, n, i).start()
 
-        @pl.when(far & here)
-        def _():
-            far_core_copy(f, n, h).wait_recv()
-            work_far[f, n, h] = add(work_far[f, n, h], core_far[f, n // 2, h])
-            far_copy(f, z, n, h, near_end).start()
+        @pl.when(far & here & wide)
+        def _():
+            join_far(f, z, n, h)
+
+        @pl.when(far & here & jnp.logical_not(wide))
+        def _():
+            for i in range(HALVES):
+                join_far(f, z, n, i)
 
     def join_chips(s, carry):
         own, far, comes, wide, z, n, f, h = decode(s)

time: 121 us -> 120 us (level)
  no operation moved by 1% of the time
where the time goes in v4:
time: 120 us
  Pallas kernels  116 us (97%)
  local copies, waits for them, and re-layouts  2.26 us (2%)
  other arithmetic  1.64 us (1%)
    pallas_call x1, Pallas kernels, body(): pl.pallas_call(functools.partial(kernel, n_row, n_col, cap, n_chunk), out...  116 us

profile of v4, /device:TPU:25, one launch (start us, length us, event | category | flops | bytes accessed | tf_op | source)
XLA Modules:
  0.0 120.2 jit_solution(7611974502137067297)
XLA Ops:
  0.0 0.7 broadcast_subtract_fusion
  0.7 0.2 convert_reduce_fusion
  1.0 0.7 select_reduce_fusion.refs_0_
  1.7 116.3 %shard_map.55 = bf16[512,1024]{1,0:T(8,128)(2,1)} custom-call(s32[80]{0:T(128)} %select_reduce_fusion.refs_0_, s32[321]{0:T(512)} %refs_1_.1, s32[4,320]{1,0:T(4,128)} %bitcast.1, bf16[40,32,1024]{2,1,0:T(8,128)(2,1)} %refs_3_.1, bf16[1280,1024]{1,0:T(8,128)(2,1)} %refs_4_.1), custom_call_target="tpu_custom_call" | custom-call | tf_op jit(solution)/shard_map/pallas_call | solution.py:584
  117.9 2.3 %copy.7 = bf16[512,1024]{1,0:T(8,128)(2,1)} copy(bf16[512,1024]{1,0:T(8,128)(2,1)} %shard_map.55) | data formatting | bytes 2097152
  (3 shorter events, 0.0 us)
